TPU v7x, 128 devices: a whole 4x4x4 slice. The times are simulated.
128 devices in a mesh: north: 32 (over z_hi, y, x), deep: 4 (over z_lo, core).
Axes of the slice: x: 4, y: 4, z: 4 (z_hi: 2, z_lo: 2; z = z_hi * 2 + z_lo), core: 2. Of those that a mesh axis runs over, the one named last changes fastest.
Arguments:
- forcing: float32 [2, 512, 512, 256], P(None, None, 'north', 'deep'), may hold values from -6 to 6
- symbol_x: float32 [512], replicated, may hold values from 0.3 to 3
- symbol_y: float32 [512], replicated, may hold values from 0.3 to 3
- symbol_z: float32 [256], replicated, may hold values from 0.3 to 3
Outputs:
- coefficients: float32 [2, 512, 512, 256], P(None, 'north', 'deep')
All inputs are finite; a program needn't handle non-finite values.
Results may differ from a plain program's by a relative error of at most 0.000084.
Values sent between devices are 32-bit elements; how exact they have to be, the bound alone decides.
A program may use at most 64 MiB of HBM per device.

v0:
```python
import functools

import jax
import jax.numpy as jnp
import ml_dtypes
import numpy as np
from jax import lax
from jax.experimental import pallas as pl
from jax.experimental.pallas import tpu as pltpu
from jax.sharding import PartitionSpec as P

MESH = pl.DeviceIdType.MESH
F32, BF16 = jnp.float32, jnp.bfloat16
SIDE = 4
PLANE = SIDE * SIDE
STEPS = ((1, 0), (0, 1), (3, 0), (0, 3), (1, 1), (3, 3), (1, 3), (3, 1), (2, 0), (0, 2), (2, 1), (1, 2), (2, 3), (3, 2), (2, 2))
PIECES = 4


def table(count):
    rank = np.arange(count, dtype=np.int64)
    turns = ((2 * rank[:, None] + 1) * (2 * rank[None, :] + 1)) % (8 * count)
    exact = np.cos(np.pi / (4 * count) * turns) * np.sqrt(2.0 / count)
    high = exact.astype(np.float32).astype(ml_dtypes.bfloat16)
    low = (exact - high.astype(np.float64)).astype(np.float32).astype(ml_dtypes.bfloat16)
    return np.stack([high, low])


def split(value):
    high = value.astype(BF16)
    return high, (value - high.astype(F32)).astype(BF16)


def dot(a, b, b_dim=0):
    return lax.dot_general(a, b, (((1,), (b_dim,)), ((), ())), preferred_element_type=F32)


def kernel(
    x_hbm, sx_hbm, sy_hbm, sz_hbm, h_hbm, hz_hbm, o_hbm,
    xin, h, hz, xo, zr, yr, yo, pr, out, sx, sy, sz, sycol,
    in_sem, tab_sem, sym_sem, z_send, z_recv, xy_send, xy_recv, p_send, p_recv, o_sem,
):
    n = lax.axis_index("north")
    d = lax.axis_index("deep")
    half, q = n // PLANE, n % PLANE
    qx, qy = q % SIDE, q // SIDE
    group = 16 // PIECES

    table_copies = [
        pltpu.make_async_copy(h_hbm, h, tab_sem.at[0]),
        pltpu.make_async_copy(hz_hbm, hz, tab_sem.at[1]),
    ]
    table_copies[0].start()

    def in_copy(g, f):
        return pltpu.make_async_copy(
            x_hbm.at[f, pl.ds(g * group, group)], xin.at[pl.ds(g * group, group), f], in_sem.at[g, f]
        )

    for g in range(PIECES):
        for f in range(2):
            in_copy(g, f).start()
    table_copies[1].start()
    symbol_copies = [
        pltpu.make_async_copy(sx_hbm, sx, sym_sem.at[0]),
        pltpu.make_async_copy(sy_hbm, sy, sym_sem.at[1]),
        pltpu.make_async_copy(sz_hbm, sz, sym_sem.at[2]),
    ]
    for copy in symbol_copies:
        copy.start()

    def plane_chip(step):
        return ((qy + step[1]) % SIDE) * SIDE + (qx + step[0]) % SIDE

    across = ((1 - half) * PLANE + q, d)
    barrier = pltpu.get_barrier_semaphore()
    for step in STEPS:
        pl.semaphore_signal(barrier, inc=1, device_id=(half * PLANE + plane_chip(step), d), device_id_type=MESH)
    pl.semaphore_signal(barrier, inc=1, device_id=across, device_id_type=MESH)
    for flip in (1, 2, 3):
        pl.semaphore_signal(barrier, inc=1, device_id=(n, d ^ flip), device_id_type=MESH)
    pl.semaphore_wait(barrier, len(STEPS) + 4)

    def z_copy(c, g):
        return pltpu.make_async_remote_copy(
            src_ref=xo.at[1, c, :, pl.ds(g * group, group)],
            dst_ref=zr.at[c, :, pl.ds(g * group, group)],
            send_sem=z_send,
            recv_sem=z_recv.at[c, g],
            device_id=across,
            device_id_type=MESH,
        )

    table_copies[0].wait()

    def x_pair(i, carry):
        value = xin[pl.ds(2 * i, 2)].reshape(256, 512)
        high, low = split(value)
        for rel in (1, 0):
            side = jnp.where(rel == 1, 1 - half, half)
            rows = pl.ds(pl.multiple_of(side * 256, 256), 256)
            a_high, a_low = h[0, rows, :], h[1, rows, :]
            res = dot(a_high, high, 1) + dot(a_low, high, 1) + dot(a_high, low, 1)
            res = res.reshape(PLANE, 2, 8, 256)
            for c in range(2):
                for y in range(2):
                    xo[rel, c, :, 2 * i + y] = res[:, c, :, 128 * y : 128 * (y + 1)]
        return carry

    for g in range(PIECES):
        for f in range(2):
            in_copy(g, f).wait()
        lax.fori_loop(g * group // 2, (g + 1) * group // 2, x_pair, 0)
        z_copy(0, g).start()
    for g in range(PIECES):
        z_copy(1, g).start()

    def xy_own(c):
        for step in STEPS:
            to = plane_chip(step)
            pltpu.make_async_remote_copy(
                src_ref=xo.at[0, c, to],
                dst_ref=yr.at[c, n],
                send_sem=xy_send,
                recv_sem=xy_recv.at[c],
                device_id=(half * PLANE + to, d),
                device_id_type=MESH,
            ).start()
        yr[c, n] = xo[0, c, q]

    from_across = (1 - half) * PLANE + q

    def xy_relay(c):
        def piece(g, carry):
            z_copy(c, g).wait_recv()
            part = pl.ds(g * group, group)
            for step in STEPS:
                to = plane_chip(step)
                pltpu.make_async_remote_copy(
                    src_ref=zr.at[c, to, part],
                    dst_ref=yr.at[c, from_across, part],
                    send_sem=xy_send,
                    recv_sem=xy_recv.at[c],
                    device_id=(half * PLANE + to, d),
                    device_id_type=MESH,
                ).start()
            return carry

        lax.fori_loop(0, PIECES, piece, 0)
        yr[c, from_across] = zr[c, q]

    def along_y(c):
        pltpu.make_async_remote_copy(
            src_ref=yr.at[c, pl.ds(0, 30)],
            dst_ref=yr.at[c, pl.ds(0, 30)],
            send_sem=xy_send,
            recv_sem=xy_recv.at[c],
            device_id=across,
            device_id_type=MESH,
        ).wait_recv()
        lines = yr.at[c].reshape(4096, 128)

        def pair(i, carry):
            value = jnp.concatenate([lines[pl.ds(2 * i + k, 512, stride=8), :] for k in range(2)], axis=1)
            high, low = split(value)
            for part in range(2):
                rows = pl.ds(part * 256, 256)
                a_high, a_low = h[0, rows, :], h[1, rows, :]
                res = dot(a_high, high) + dot(a_low, high) + dot(a_high, low)
                for k in range(2):
                    for s in range(2):
                        yo[c, 2 * part + s, 2 * i + k] = res[128 * s : 128 * (s + 1), 128 * k : 128 * (k + 1)]
            for k in range(2):
                pr[c, d, 2 * i + k] = yo[c, d, 2 * i + k]
                for flip in (2, 3, 1):
                    pltpu.make_async_remote_copy(
                        src_ref=yo.at[c, d ^ flip, 2 * i + k],
                        dst_ref=pr.at[c, d, 2 * i + k],
                        send_sem=p_send,
                        recv_sem=p_recv.at[c, 2 * i + k],
                        device_id=(n, d ^ flip),
                        device_id_type=MESH,
                    ).start()
            return carry

        lax.fori_loop(0, 4, pair, 0)

    def along_z(c):
        first = lax.broadcasted_iota(jnp.int32, (128, 128), 1) < 64

        def line(j, carry):
            pltpu.make_async_remote_copy(
                src_ref=pr.at[c, pl.ds(0, 3), 0],
                dst_ref=pr.at[c, pl.ds(0, 3), 0],
                send_sem=p_send,
                recv_sem=p_recv.at[c, j],
                device_id=across,
                device_id_type=MESH,
            ).wait_recv()
            parts = [pr[c, s, j] for s in range(4)]
            turned = [pltpu.roll(p, 64, 1) for p in parts]
            field = [
                jnp.concatenate([jnp.where(first, parts[s], turned[s + 1]) for s in (0, 2)], axis=1),
                jnp.concatenate([jnp.where(first, turned[s], parts[s + 1]) for s in (0, 2)], axis=1),
            ]
            high, low = split(jnp.concatenate(field, axis=0))
            res = dot(high, hz[0]) + dot(high, hz[1]) + dot(low, hz[0])
            symbol = (sx[n * 16 + c * 8 + j] + sycol[...]) + sz[...]
            factor = (1.0 - 0.2 * symbol) / (1.0 + 0.2 * symbol)
            for f in range(2):
                out[f, c * 8 + j] = res[128 * f : 128 * (f + 1)] * factor
            pltpu.make_async_copy(out.at[:, c * 8 + j], o_hbm.at[:, c * 8 + j], o_sem).start()
            return carry

        lax.fori_loop(0, 8, line, 0)

    xy_own(0)
    xy_relay(0)
    xy_own(1)
    for copy in symbol_copies:
        copy.wait()
    table_copies[1].wait()
    along = sy[pl.ds(d, 1), :]
    sycol[...] = jnp.concatenate([jnp.transpose(jnp.broadcast_to(along, (128, 128)))] * 2, axis=1)
    along_y(0)
    xy_relay(1)
    along_y(1)
    along_z(0)
    along_z(1)

    def drain(ref, sem):
        pltpu.make_async_remote_copy(
            src_ref=ref, dst_ref=ref, send_sem=sem, recv_sem=p_recv.at[0, 0], device_id=across, device_id_type=MESH
        ).wait_send()

    drain(zr, z_send)
    for c in range(2):
        drain(yr.at[c, pl.ds(0, 30)], xy_send)
        drain(pr.at[c, pl.ds(0, 3)], p_send)
    pltpu.make_async_copy(out, o_hbm, o_sem).wait()


def local(forcing, symbol_x, symbol_y, symbol_z):
    lines = jnp.transpose(forcing, (0, 2, 3, 1))
    return pl.pallas_call(
        kernel,
        out_shape=jax.ShapeDtypeStruct((2, 16, 128, 256), F32),
        in_specs=[pl.BlockSpec(memory_space=pl.ANY)] * 6,
        out_specs=pl.BlockSpec(memory_space=pl.ANY),
        scratch_shapes=[
            pltpu.VMEM((16, 2, 64, 512), F32),
            pltpu.VMEM((2, 512, 512), BF16),
            pltpu.VMEM((2, 256, 256), BF16),
            pltpu.VMEM((2, 2, 16, 16, 8, 128), F32),
            pltpu.VMEM((2, 16, 16, 8, 128), F32),
            pltpu.VMEM((2, 32, 16, 8, 128), F32),
            pltpu.VMEM((2, 4, 8, 128, 128), F32),
            pltpu.VMEM((2, 4, 8, 128, 128), F32),
            pltpu.VMEM((2, 16, 128, 256), F32),
            pltpu.SMEM((512,), F32),
            pltpu.VMEM((4, 128), F32),
            pltpu.VMEM((1, 256), F32),
            pltpu.VMEM((128, 256), F32),
            pltpu.SemaphoreType.DMA((PIECES, 2)),
            pltpu.SemaphoreType.DMA((2,)),
            pltpu.SemaphoreType.DMA((3,)),
            pltpu.SemaphoreType.DMA,
            pltpu.SemaphoreType.DMA((2, PIECES)),
            pltpu.SemaphoreType.DMA,
            pltpu.SemaphoreType.DMA((2,)),
            pltpu.SemaphoreType.DMA,
            pltpu.SemaphoreType.DMA((2, 8)),
            pltpu.SemaphoreType.DMA,
        ],
        compiler_params=pltpu.CompilerParams(
            collective_id=0, has_side_effects=True, vmem_limit_bytes=48 * 2**20
        ),
        name="transform",
    )(
        lines, symbol_x, symbol_y.reshape(4, 128), symbol_z.reshape(1, 256),
        jnp.asarray(table(512)), jnp.asarray(table(256)),
    )


def solution(mesh):
    return jax.shard_map(
        local,
        mesh=mesh,
        in_specs=(P(None, None, "north", "deep"), P(), P(), P()),
        out_specs=P(None, "north", "deep", None),
        check_vma=False,
    )
```

profile of v0, /device:TPU:1, one launch (start us, length us, event | category | flops | bytes accessed | tf_op | source)
XLA Modules:
  0.0 107.1 jit_solution(1918008745429853362)
XLA Ops:
  0.0 0.0 copy-start
  0.0 1.2 %copy-done = bf16[2,512,512]{2,1,0:T(8,128)(2,1)S(1)} copy-done((bf16[2,512,512]{2,1,0:T(8,128)(2,1)S(1)}, bf16[2,512,512]{2,1,0:T(8,128)(2,1)}, u32[]{:S(2)}) %copy-start) | copy-done | bytes 1048600
  1.2 0.0 copy-start.1
  1.2 0.9 copy-done.1
  2.2 0.0 copy-start.2
  2.2 0.7 copy-done.2
  2.9 0.0 copy-start.3
  2.9 0.7 copy-done.3
  3.5 0.0 copy-start.4
  3.5 0.7 copy-done.4
  4.2 100.9 %transform.1 = f32[2,16,128,256]{3,2,1,0:T(8,128)S(1)} custom-call(f32[2,16,64,512]{3,2,1,0:T(8,128)} %bitcast.5, f32[512]{0:T(512)S(1)} %copy-done.2, f32[4,128]{1,0:T(4,128)S(1)} %bitcast.3, f32[1,256]{1,0:T(1,128)S(1)} %bitcast.4, bf16[2,512,512]{2,1,0:T(8,128)(2,1)S(1)} %copy-done, bf16[2,256,256]{2,1,0:T(8,128)(2,1)S(1)} %copy-done.1), custom_call_target="tpu_custom_call" | custom-call | tf_op jit(solution)/shard_map/transform/pallas_call | solution.py:245
  105.1 2.0 %copy.8 = f32[2,16,128,256]{3,2,1,0:T(8,128)} copy(f32[2,16,128,256]{3,2,1,0:T(8,128)S(1)} %transform.1) | data formatting | bytes 8388608
Async XLA Ops:
  0.0 1.2 %copy-start = (bf16[2,512,512]{2,1,0:T(8,128)(2,1)S(1)}, bf16[2,512,512]{2,1,0:T(8,128)(2,1)}, u32[]{:S(2)}) copy-start(bf16[2,512,512]{2,1,0:T(8,128)(2,1)} %constant.4.clone.h_hbm) | copy-start | bytes 3145732
  1.2 0.9 copy-start.1
  2.2 0.7 copy-start.2
  2.9 0.7 copy-start.3
  3.5 0.7 copy-start.4
where the time goes:
time: 107 us
  Pallas kernels  101 us (94%)
  local copies, waits for them, and re-layouts  6.23 us (6%)
    pallas_call x1, Pallas kernels, local(): pl.pallas_call(kernel, out_shape=jax.ShapeDtypeStruct((2, 16, 128, 256),...  101 us
    unnamed x11, local copies, waits for them, and re-layouts  6.23 us

commit v1 on v0

--- a/solution.py
+++ b/solution.py
@@ -14,6 +14,7 @@
 SIDE = 4
 PLANE = SIDE * SIDE
 STEPS = ((1, 0), (0, 1), (3, 0), (0, 3), (1, 1), (3, 3), (1, 3), (3, 1), (2, 0), (0, 2), (2, 1), (1, 2), (2, 3), (3, 2), (2, 2))
+LINE = tuple(step for step in STEPS if 0 in step)
 PIECES = 4
 
 
@@ -36,9 +37,9 @@
 
 
 def kernel(
-    x_hbm, sx_hbm, sy_hbm, sz_hbm, h_hbm, hz_hbm, o_hbm,
-    xin, h, hz, xo, zr, yr, yo, pr, out, sx, sy, sz, sycol,
-    in_sem, tab_sem, sym_sem, z_send, z_recv, xy_send, xy_recv, p_send, p_recv, o_sem,
+    x_hbm, sx_hbm, sy_hbm, sz_hbm, h_hbm, hz_hbm, out,
+    xin, h, hz, xo, zr, yr, yo, pr, sx, sy, sz, sycol,
+    in_sem, tab_sem, sym_sem, z_send, z_recv, xy_send, xy_recv, p_send, p_recv, ready,
 ):
     n = lax.axis_index("north")
     d = lax.axis_index("deep")
@@ -52,14 +53,12 @@
     ]
     table_copies[0].start()
 
-    def in_copy(g, f):
-        return pltpu.make_async_copy(
-            x_hbm.at[f, pl.ds(g * group, group)], xin.at[pl.ds(g * group, group), f], in_sem.at[g, f]
-        )
-
-    for g in range(PIECES):
+    def in_copy(i, f):
+        return pltpu.make_async_copy(x_hbm.at[f, pl.ds(2 * i, 2)], xin.at[pl.ds(2 * i, 2), f], in_sem.at[i, f])
+
+    for i in range(8):
         for f in range(2):
-            in_copy(g, f).start()
+            in_copy(i, f).start()
     table_copies[1].start()
     symbol_copies = [
         pltpu.make_async_copy(sx_hbm, sx, sym_sem.at[0]),
@@ -74,19 +73,19 @@
 
     across = ((1 - half) * PLANE + q, d)
     barrier = pltpu.get_barrier_semaphore()
-    for step in STEPS:
+    pl.semaphore_signal(barrier, inc=1, device_id=across, device_id_type=MESH)
+    for step in LINE:
         pl.semaphore_signal(barrier, inc=1, device_id=(half * PLANE + plane_chip(step), d), device_id_type=MESH)
-    pl.semaphore_signal(barrier, inc=1, device_id=across, device_id_type=MESH)
     for flip in (1, 2, 3):
         pl.semaphore_signal(barrier, inc=1, device_id=(n, d ^ flip), device_id_type=MESH)
-    pl.semaphore_wait(barrier, len(STEPS) + 4)
-
-    def z_copy(c, g):
+
+    def z_copy(c, i, count):
+        part = pl.ds(i, count)
         return pltpu.make_async_remote_copy(
-            src_ref=xo.at[1, c, :, pl.ds(g * group, group)],
-            dst_ref=zr.at[c, :, pl.ds(g * group, group)],
+            src_ref=xo.at[1, c, :, part],
+            dst_ref=zr.at[c, :, part],
             send_sem=z_send,
-            recv_sem=z_recv.at[c, g],
+            recv_sem=z_recv.at[c, i // group],
             device_id=across,
             device_id_type=MESH,
         )
@@ -107,13 +106,25 @@
                     xo[rel, c, :, 2 * i + y] = res[:, c, :, 128 * y : 128 * (y + 1)]
         return carry
 
+    def x_step(i, carry):
+        for f in range(2):
+            in_copy(i, f).wait()
+        x_pair(i, carry)
+        z_copy(0, 2 * i, 2).start()
+        return carry
+
+    for f in range(2):
+        in_copy(0, f).wait()
+    x_pair(0, 0)
+    pl.semaphore_wait(barrier, len(LINE) + 4)
+    z_copy(0, 0, 2).start()
+    for step in LINE:
+        if step[1] == 0:
+            pl.semaphore_signal(ready, inc=1, device_id=(half * PLANE + plane_chip(step), d), device_id_type=MESH)
+    lax.fori_loop(1, 8, x_step, 0)
     for g in range(PIECES):
-        for f in range(2):
-            in_copy(g, f).wait()
-        lax.fori_loop(g * group // 2, (g + 1) * group // 2, x_pair, 0)
-        z_copy(0, g).start()
-    for g in range(PIECES):
-        z_copy(1, g).start()
+        z_copy(1, g * group, group).start()
+    pl.semaphore_wait(ready, SIDE - 1)
 
     def xy_own(c):
         for step in STEPS:
@@ -132,7 +143,7 @@
 
     def xy_relay(c):
         def piece(g, carry):
-            z_copy(c, g).wait_recv()
+            z_copy(c, g * group, group).wait_recv()
             part = pl.ds(g * group, group)
             for step in STEPS:
                 to = plane_chip(step)
@@ -209,7 +220,6 @@
             factor = (1.0 - 0.2 * symbol) / (1.0 + 0.2 * symbol)
             for f in range(2):
                 out[f, c * 8 + j] = res[128 * f : 128 * (f + 1)] * factor
-            pltpu.make_async_copy(out.at[:, c * 8 + j], o_hbm.at[:, c * 8 + j], o_sem).start()
             return carry
 
         lax.fori_loop(0, 8, line, 0)
@@ -237,7 +247,6 @@
     for c in range(2):
         drain(yr.at[c, pl.ds(0, 30)], xy_send)
         drain(pr.at[c, pl.ds(0, 3)], p_send)
-    pltpu.make_async_copy(out, o_hbm, o_sem).wait()
 
 
 def local(forcing, symbol_x, symbol_y, symbol_z):
@@ -245,8 +254,8 @@
     return pl.pallas_call(
         kernel,
         out_shape=jax.ShapeDtypeStruct((2, 16, 128, 256), F32),
-        in_specs=[pl.BlockSpec(memory_space=pl.ANY)] * 6,
-        out_specs=pl.BlockSpec(memory_space=pl.ANY),
+        in_specs=[pl.BlockSpec(memory_space=pltpu.HBM)] * 6,
+        out_specs=pl.BlockSpec(memory_space=pltpu.VMEM),
         scratch_shapes=[
             pltpu.VMEM((16, 2, 64, 512), F32),
             pltpu.VMEM((2, 512, 512), BF16),
@@ -256,12 +265,11 @@
             pltpu.VMEM((2, 32, 16, 8, 128), F32),
             pltpu.VMEM((2, 4, 8, 128, 128), F32),
             pltpu.VMEM((2, 4, 8, 128, 128), F32),
-            pltpu.VMEM((2, 16, 128, 256), F32),
             pltpu.SMEM((512,), F32),
             pltpu.VMEM((4, 128), F32),
             pltpu.VMEM((1, 256), F32),
             pltpu.VMEM((128, 256), F32),
-            pltpu.SemaphoreType.DMA((PIECES, 2)),
+            pltpu.SemaphoreType.DMA((8, 2)),
             pltpu.SemaphoreType.DMA((2,)),
             pltpu.SemaphoreType.DMA((3,)),
             pltpu.SemaphoreType.DMA,
@@ -270,15 +278,24 @@
             pltpu.SemaphoreType.DMA((2,)),
             pltpu.SemaphoreType.DMA,
             pltpu.SemaphoreType.DMA((2, 8)),
-            pltpu.SemaphoreType.DMA,
+            pltpu.SemaphoreType.REGULAR,
         ],
         compiler_params=pltpu.CompilerParams(
             collective_id=0, has_side_effects=True, vmem_limit_bytes=48 * 2**20
         ),
         name="transform",
     )(
-        lines, symbol_x, symbol_y.reshape(4, 128), symbol_z.reshape(1, 256),
-        jnp.asarray(table(512)), jnp.asarray(table(256)),
+        *(
+            pltpu.with_memory_space_constraint(value, pltpu.HBM)
+            for value in (
+                lines,
+                symbol_x,
+                symbol_y.reshape(4, 128),
+                symbol_z.reshape(1, 256),
+                jnp.asarray(table(512)),
+                jnp.asarray(table(256)),
+            )
+        )
     )
 
 

time: 107 us -> 99.2 us (0.927)
  local copies, waits for them, and re-layouts: 6.23 us -> 2.02 us
  Pallas kernels: 101 us -> 97.1 us
    unnamed x11 -> x1, local copies, waits for them, and re-layouts: 6.23 us -> 2.02 us
    pallas_call x1, Pallas kernels: 101 us -> 97.1 us  [local(): pl.pallas_call(kernel, out_shape=jax.ShapeDtypeStruct((2, 16, 128, 256),...]
where the time goes in v1:
time: 99.2 us; the launch traced here: 99.1 us
  Pallas kernels  97.1 us (98%)
  local copies, waits for them, and re-layouts  2.02 us (2%)
    pallas_call x1, Pallas kernels, local(): pl.pallas_call(kernel, out_shape=jax.ShapeDtypeStruct((2, 16, 128, 256),...  97.1 us
    unnamed x1, local copies, waits for them, and re-layouts  2.02 us

profile of v1, /device:TPU:1, one launch (start us, length us, event | category | flops | bytes accessed | tf_op | source)
XLA Modules:
  0.0 99.1 jit_solution(11421792461234834549)
XLA Ops:
  0.0 97.1 %transform.1 = f32[2,16,128,256]{3,2,1,0:T(8,128)S(1)} custom-call(f32[2,16,64,512]{3,2,1,0:T(8,128)} %bitcast.3, f32[512]{0:T(512)} %sx_hbm.1, f32[4,128]{1,0:T(4,128)} %bitcast.4, f32[1,256]{1,0:T(1,128)} %bitcast.5, bf16[2,512,512]{2,1,0:T(8,128)(2,1)} %constant.4.clone.h_hbm, bf16[2,256,256]{2,1,0:T(8,128)(2,1)} %constant.5.clone.hz_hbm), custom_call_target="tpu_custom_call" | custom-call | tf_op jit(solution)/shard_map/transform/pallas_call | solution.py:254
  97.1 2.0 %copy.8 = f32[2,16,128,256]{3,2,1,0:T(8,128)} copy(f32[2,16,128,256]{3,2,1,0:T(8,128)S(1)} %transform.1) | data formatting | bytes 8388608

commit v2 on v1

--- a/solution.py
+++ b/solution.py
@@ -17,6 +17,8 @@
 LINE = tuple(step for step in STEPS if 0 in step)
 PIECES = 4
 
+LINES = (2, 1)
+
 
 def table(count):
     rank = np.arange(count, dtype=np.int64)
@@ -38,8 +40,8 @@
 
 def kernel(
     x_hbm, sx_hbm, sy_hbm, sz_hbm, h_hbm, hz_hbm, out,
-    xin, h, hz, xo, zr, yr, yo, pr, sx, sy, sz, sycol,
-    in_sem, tab_sem, sym_sem, z_send, z_recv, xy_send, xy_recv, p_send, p_recv, ready,
+    xin, h, hz, xo, zr, yr, yo, pr, fw, via, sx, sy, sz, sycol, factor,
+    in_sem, tab_sem, sym_sem, z_send, z_recv, xy_send, xy_recv, p_send, p_recv, f_send, f_recv, v_sem, near, far, row, column,
 ):
     n = lax.axis_index("north")
     d = lax.axis_index("deep")
@@ -47,37 +49,53 @@
     qx, qy = q % SIDE, q // SIDE
     group = 16 // PIECES
 
-    table_copies = [
-        pltpu.make_async_copy(h_hbm, h, tab_sem.at[0]),
-        pltpu.make_async_copy(hz_hbm, hz, tab_sem.at[1]),
-    ]
-    table_copies[0].start()
+    def table_copy(rel):
+        side = jnp.where(rel == 1, 1 - half, half)
+        rows = pl.ds(pl.multiple_of(side * 256, 256), 256)
+        return pltpu.make_async_copy(h_hbm.at[:, rows], h.at[:, rows], tab_sem.at[rel])
+
+    hz_copy = pltpu.make_async_copy(hz_hbm, hz, tab_sem.at[2])
+    table_copy(1).start()
 
     def in_copy(i, f):
-        return pltpu.make_async_copy(x_hbm.at[f, pl.ds(2 * i, 2)], xin.at[pl.ds(2 * i, 2), f], in_sem.at[i, f])
-
-    for i in range(8):
-        for f in range(2):
-            in_copy(i, f).start()
-    table_copies[1].start()
+        return pltpu.make_async_copy(x_hbm.at[f, pl.ds(2 * i, 2)], xin.at[pl.ds(2 * i, 2), f], in_sem.at[min(i, 1)])
+
+    for f in range(2):
+        in_copy(0, f).start()
     symbol_copies = [
         pltpu.make_async_copy(sx_hbm, sx, sym_sem.at[0]),
         pltpu.make_async_copy(sy_hbm, sy, sym_sem.at[1]),
         pltpu.make_async_copy(sz_hbm, sz, sym_sem.at[2]),
     ]
-    for copy in symbol_copies:
-        copy.start()
 
     def plane_chip(step):
         return ((qy + step[1]) % SIDE) * SIDE + (qx + step[0]) % SIDE
 
     across = ((1 - half) * PLANE + q, d)
+    mate, twin, beyond = (n, d ^ 2), (n, d ^ 1), ((1 - half) * PLANE + q, d ^ 2)
+    middle = half != d // 2
+    outer = half == d // 2
+
+    def tell(semaphore, to):
+        pl.semaphore_signal(semaphore, inc=1, device_id=to, device_id_type=MESH)
+
     barrier = pltpu.get_barrier_semaphore()
-    pl.semaphore_signal(barrier, inc=1, device_id=across, device_id_type=MESH)
-    for step in LINE:
-        pl.semaphore_signal(barrier, inc=1, device_id=(half * PLANE + plane_chip(step), d), device_id_type=MESH)
-    for flip in (1, 2, 3):
-        pl.semaphore_signal(barrier, inc=1, device_id=(n, d ^ flip), device_id_type=MESH)
+    for peer in (mate, twin):
+        tell(barrier, peer)
+    pl.when(middle)(lambda: tell(barrier, beyond))
+    pl.when(qx > 0)(lambda: tell(barrier, (n - 1, d)))
+    pl.when(qx < SIDE - 1)(lambda: tell(barrier, (n + 1, d)))
+    pl.when(qy > 0)(lambda: tell(barrier, (n - SIDE, d)))
+    pl.when(qy < SIDE - 1)(lambda: tell(barrier, (n + SIDE, d)))
+    contacts = 2 + middle.astype(jnp.int32)
+    for at in (qx, qy):
+        contacts += (at > 0).astype(jnp.int32) + (at < SIDE - 1).astype(jnp.int32)
+
+    def sweep(sems, at, stride):
+        pl.when(at > 0)(lambda: pl.semaphore_wait(sems.at[0], 1))
+        pl.when(at < SIDE - 1)(lambda: tell(sems.at[0], (n + stride, d)))
+        pl.when(at < SIDE - 1)(lambda: pl.semaphore_wait(sems.at[1], 1))
+        pl.when(at > 0)(lambda: tell(sems.at[1], (n - stride, d)))
 
     def z_copy(c, i, count):
         part = pl.ds(i, count)
@@ -90,11 +108,21 @@
             device_id_type=MESH,
         )
 
-    table_copies[0].wait()
-
-    def x_pair(i, carry):
+
+    def x_half(i, rel):
         value = xin[pl.ds(2 * i, 2)].reshape(256, 512)
         high, low = split(value)
+        side = jnp.where(rel == 1, 1 - half, half)
+        rows = pl.ds(pl.multiple_of(side * 256, 256), 256)
+        a_high, a_low = h[0, rows, :], h[1, rows, :]
+        res = dot(a_high, high, 1) + dot(a_low, high, 1) + dot(a_high, low, 1)
+        res = res.reshape(PLANE, 2, 8, 256)
+        for c in range(2):
+            for y in range(2):
+                xo[rel, c, :, 2 * i + y] = res[:, c, :, 128 * y : 128 * (y + 1)]
+
+    def x_pair(i):
+        high, low = split(xin[pl.ds(2 * i, 2)].reshape(256, 512))
         for rel in (1, 0):
             side = jnp.where(rel == 1, 1 - half, half)
             rows = pl.ds(pl.multiple_of(side * 256, 256), 256)
@@ -104,27 +132,64 @@
             for c in range(2):
                 for y in range(2):
                     xo[rel, c, :, 2 * i + y] = res[:, c, :, 128 * y : 128 * (y + 1)]
-        return carry
 
     def x_step(i, carry):
-        for f in range(2):
-            in_copy(i, f).wait()
-        x_pair(i, carry)
+        x_pair(i)
         z_copy(0, 2 * i, 2).start()
         return carry
 
-    for f in range(2):
-        in_copy(0, f).wait()
-    x_pair(0, 0)
-    pl.semaphore_wait(barrier, len(LINE) + 4)
+    first_copy = pltpu.make_async_remote_copy(
+        src_ref=xo.at[1, 1, :, pl.ds(0, 2)],
+        dst_ref=via,
+        send_sem=v_sem.at[0],
+        recv_sem=v_sem.at[1],
+        device_id=mate,
+        device_id_type=MESH,
+    )
+    onward_copy = pltpu.make_async_remote_copy(
+        src_ref=via,
+        dst_ref=zr.at[1, :, pl.ds(0, 2)],
+        send_sem=z_send,
+        recv_sem=z_recv.at[1, 0],
+        device_id=beyond,
+        device_id_type=MESH,
+    )
+    def in_wait(planes, k):
+        pltpu.make_async_copy(xin.at[planes], xin.at[planes], in_sem.at[k]).wait()
+
+    table_copy(1).wait()
+    in_wait(pl.ds(0, 2), 0)
+    table_copy(0).start()
+    for i in range(1, 8):
+        for f in range(2):
+            in_copy(i, f).start()
+    for copy in [hz_copy, *symbol_copies]:
+        copy.start()
+    x_half(0, 1)
+    pl.semaphore_wait(barrier, contacts)
+    first_copy.start()
+    @pl.when(middle)
+    def _():
+        tell(near, mate)
+        tell(near, beyond)
+
+    table_copy(0).wait()
+    x_half(0, 0)
+    pl.semaphore_wait(near, 1)
     z_copy(0, 0, 2).start()
-    for step in LINE:
-        if step[1] == 0:
-            pl.semaphore_signal(ready, inc=1, device_id=(half * PLANE + plane_chip(step), d), device_id_type=MESH)
-    lax.fori_loop(1, 8, x_step, 0)
-    for g in range(PIECES):
+    pl.when(middle)(lambda: tell(far, across))
+    in_wait(pl.ds(2, 14), 1)
+    lax.fori_loop(1, 4, x_step, 0)
+    sweep(row, qx, 1)
+    lax.fori_loop(4, 7, x_step, 0)
+    sweep(column, qy, SIDE)
+    x_step(7, 0)
+    first_copy.wait_recv()
+    pl.when(outer)(lambda: pl.semaphore_wait(far, 1))
+    onward_copy.start()
+    z_copy(1, 2, 2).start()
+    for g in range(1, PIECES):
         z_copy(1, g * group, group).start()
-    pl.semaphore_wait(ready, SIDE - 1)
 
     def xy_own(c):
         for step in STEPS:
@@ -142,7 +207,8 @@
     from_across = (1 - half) * PLANE + q
 
     def xy_relay(c):
-        def piece(g, carry):
+        def piece(k, carry):
+            g = (k + c) % PIECES
             z_copy(c, g * group, group).wait_recv()
             part = pl.ds(g * group, group)
             for step in STEPS:
@@ -160,6 +226,36 @@
         lax.fori_loop(0, PIECES, piece, 0)
         yr[c, from_across] = zr[c, q]
 
+    def firsts(c):
+        return range(0, 2, LINES[c])
+
+    def p_copy(ref, source, c, j, to):
+        part = pl.ds(j, LINES[c])
+        return pltpu.make_async_remote_copy(
+            src_ref=ref.at[part],
+            dst_ref=pr.at[c, source, part],
+            send_sem=p_send,
+            recv_sem=p_recv.at[c * 4 + j // LINES[c]],
+            device_id=(n, to),
+            device_id_type=MESH,
+        )
+
+    def to_twin(c, i):
+        part = pl.ds(2 * i, 2)
+        return pltpu.make_async_remote_copy(
+            src_ref=yo.at[c, d ^ 3, part],
+            dst_ref=fw.at[c, part],
+            send_sem=f_send,
+            recv_sem=f_recv.at[c * 4 + i],
+            device_id=(n, d ^ 1),
+            device_id_type=MESH,
+        )
+
+    def onward(c, i):
+        to_twin(c, i).wait_recv()
+        for j in firsts(c):
+            p_copy(fw.at[c], d ^ 1, c, 2 * i + j, d ^ 2).start()
+
     def along_y(c):
         pltpu.make_async_remote_copy(
             src_ref=yr.at[c, pl.ds(0, 30)],
@@ -181,33 +277,40 @@
                 for k in range(2):
                     for s in range(2):
                         yo[c, 2 * part + s, 2 * i + k] = res[128 * s : 128 * (s + 1), 128 * k : 128 * (k + 1)]
-            for k in range(2):
-                pr[c, d, 2 * i + k] = yo[c, d, 2 * i + k]
-                for flip in (2, 3, 1):
-                    pltpu.make_async_remote_copy(
-                        src_ref=yo.at[c, d ^ flip, 2 * i + k],
-                        dst_ref=pr.at[c, d, 2 * i + k],
-                        send_sem=p_send,
-                        recv_sem=p_recv.at[c, 2 * i + k],
-                        device_id=(n, d ^ flip),
-                        device_id_type=MESH,
-                    ).start()
+            pr[c, d, pl.ds(2 * i, 2)] = yo[c, d, pl.ds(2 * i, 2)]
+            to_twin(c, i).start()
+            for j in firsts(c):
+                p_copy(yo.at[c, d ^ 1], d, c, 2 * i + j, d ^ 1).start()
+                p_copy(yo.at[c, d ^ 2], d, c, 2 * i + j, d ^ 2).start()
+
+            @pl.when(i > 0)
+            def _():
+                onward(c, i - 1)
+
             return carry
 
         lax.fori_loop(0, 4, pair, 0)
+        onward(c, 3)
 
     def along_z(c):
         first = lax.broadcasted_iota(jnp.int32, (128, 128), 1) < 64
 
         def line(j, carry):
-            pltpu.make_async_remote_copy(
-                src_ref=pr.at[c, pl.ds(0, 3), 0],
-                dst_ref=pr.at[c, pl.ds(0, 3), 0],
-                send_sem=p_send,
-                recv_sem=p_recv.at[c, j],
-                device_id=across,
-                device_id_type=MESH,
-            ).wait_recv()
+            symbol = (sx[n * 16 + c * 8 + j] + sycol[...]) + sz[...]
+            factor[...] = (1.0 - 0.2 * symbol) / (1.0 + 0.2 * symbol)
+
+            @pl.when(j % LINES[c] == 0)
+            def _():
+                whole = pr.at[c, pl.ds(0, 3), pl.ds(0, LINES[c])]
+                pltpu.make_async_remote_copy(
+                    src_ref=whole,
+                    dst_ref=whole,
+                    send_sem=p_send,
+                    recv_sem=p_recv.at[c * 4 + j // LINES[c]],
+                    device_id=across,
+                    device_id_type=MESH,
+                ).wait_recv()
+
             parts = [pr[c, s, j] for s in range(4)]
             turned = [pltpu.roll(p, 64, 1) for p in parts]
             field = [
@@ -216,10 +319,8 @@
             ]
             high, low = split(jnp.concatenate(field, axis=0))
             res = dot(high, hz[0]) + dot(high, hz[1]) + dot(low, hz[0])
-            symbol = (sx[n * 16 + c * 8 + j] + sycol[...]) + sz[...]
-            factor = (1.0 - 0.2 * symbol) / (1.0 + 0.2 * symbol)
             for f in range(2):
-                out[f, c * 8 + j] = res[128 * f : 128 * (f + 1)] * factor
+                out[f, c * 8 + j] = res[128 * f : 128 * (f + 1)] * factor[...]
             return carry
 
         lax.fori_loop(0, 8, line, 0)
@@ -229,7 +330,7 @@
     xy_own(1)
     for copy in symbol_copies:
         copy.wait()
-    table_copies[1].wait()
+    hz_copy.wait()
     along = sy[pl.ds(d, 1), :]
     sycol[...] = jnp.concatenate([jnp.transpose(jnp.broadcast_to(along, (128, 128)))] * 2, axis=1)
     along_y(0)
@@ -240,13 +341,15 @@
 
     def drain(ref, sem):
         pltpu.make_async_remote_copy(
-            src_ref=ref, dst_ref=ref, send_sem=sem, recv_sem=p_recv.at[0, 0], device_id=across, device_id_type=MESH
+            src_ref=ref, dst_ref=ref, send_sem=sem, recv_sem=p_recv.at[0], device_id=across, device_id_type=MESH
         ).wait_send()
 
+    first_copy.wait_send()
     drain(zr, z_send)
     for c in range(2):
         drain(yr.at[c, pl.ds(0, 30)], xy_send)
         drain(pr.at[c, pl.ds(0, 3)], p_send)
+        drain(fw.at[c], f_send)
 
 
 def local(forcing, symbol_x, symbol_y, symbol_z):
@@ -265,20 +368,29 @@
             pltpu.VMEM((2, 32, 16, 8, 128), F32),
             pltpu.VMEM((2, 4, 8, 128, 128), F32),
             pltpu.VMEM((2, 4, 8, 128, 128), F32),
+            pltpu.VMEM((2, 8, 128, 128), F32),
+            pltpu.VMEM((16, 2, 8, 128), F32),
             pltpu.SMEM((512,), F32),
             pltpu.VMEM((4, 128), F32),
             pltpu.VMEM((1, 256), F32),
             pltpu.VMEM((128, 256), F32),
-            pltpu.SemaphoreType.DMA((8, 2)),
+            pltpu.VMEM((128, 256), F32),
             pltpu.SemaphoreType.DMA((2,)),
+            pltpu.SemaphoreType.DMA((3,)),
             pltpu.SemaphoreType.DMA((3,)),
             pltpu.SemaphoreType.DMA,
             pltpu.SemaphoreType.DMA((2, PIECES)),
             pltpu.SemaphoreType.DMA,
             pltpu.SemaphoreType.DMA((2,)),
             pltpu.SemaphoreType.DMA,
-            pltpu.SemaphoreType.DMA((2, 8)),
+            pltpu.SemaphoreType.DMA((12,)),
+            pltpu.SemaphoreType.DMA,
+            pltpu.SemaphoreType.DMA((8,)),
+            pltpu.SemaphoreType.DMA((2,)),
             pltpu.SemaphoreType.REGULAR,
+            pltpu.SemaphoreType.REGULAR,
+            pltpu.SemaphoreType.REGULAR((2,)),
+            pltpu.SemaphoreType.REGULAR((2,)),
         ],
         compiler_params=pltpu.CompilerParams(
             collective_id=0, has_side_effects=True, vmem_limit_bytes=48 * 2**20

time: 99.2 us -> 97.7 us (0.985)
  Pallas kernels: 97.1 us -> 95.5 us
    pallas_call x1, Pallas kernels: 97.1 us -> 95.5 us  [local(): pl.pallas_call(kernel, out_shape=jax.ShapeDtypeStruct((2, 16, 128, 256),...]
where the time goes in v2:
time: 97.7 us; the launch traced here: 97.5 us
  Pallas kernels  95.5 us (98%)
  local copies, waits for them, and re-layouts  2.02 us (2%)
    pallas_call x1, Pallas kernels, local(): pl.pallas_call(kernel, out_shape=jax.ShapeDtypeStruct((2, 16, 128, 256),...  95.5 us
    unnamed x1, local copies, waits for them, and re-layouts  2.02 us

profile of v2, /device:TPU:1, one launch (start us, length us, event | category | flops | bytes accessed | tf_op | source)
XLA Modules:
  0.0 97.5 jit_solution(14751078403496560900)
XLA Ops:
  0.0 95.5 %transform.1 = f32[2,16,128,256]{3,2,1,0:T(8,128)S(1)} custom-call(f32[2,16,64,512]{3,2,1,0:T(8,128)} %bitcast.3, f32[512]{0:T(512)} %sx_hbm.1, f32[4,128]{1,0:T(4,128)} %bitcast.4, f32[1,256]{1,0:T(1,128)} %bitcast.5, bf16[2,512,512]{2,1,0:T(8,128)(2,1)} %constant.4.clone.h_hbm, bf16[2,256,256]{2,1,0:T(8,128)(2,1)} %constant.5.clone.hz_hbm), custom_call_target="tpu_custom_call" | custom-call | tf_op jit(solution)/shard_map/transform/pallas_call | solution.py:357
  95.5 2.0 %copy.8 = f32[2,16,128,256]{3,2,1,0:T(8,128)} copy(f32[2,16,128,256]{3,2,1,0:T(8,128)S(1)} %transform.1) | data formatting | bytes 8388608

commit v3 on v2

--- a/solution.py
+++ b/solution.py
@@ -29,6 +29,11 @@
     return np.stack([high, low])
 
 
+def by_chunk(rows):
+    parts = rows.reshape(2, 2, PLANE, 2, 8, rows.shape[-1])
+    return np.ascontiguousarray(parts.transpose(0, 1, 3, 2, 4, 5)).reshape(rows.shape)
+
+
 def split(value):
     high = value.astype(BF16)
     return high, (value - high.astype(F32)).astype(BF16)
@@ -38,10 +43,34 @@
     return lax.dot_general(a, b, (((1,), (b_dim,)), ((), ())), preferred_element_type=F32)
 
 
+def z_line(parts, hz):
+    first = lax.broadcasted_iota(jnp.int32, (128, 128), 1) < 64
+    turned = [pltpu.roll(p, 64, 1) for p in parts]
+    field = [
+        jnp.concatenate([jnp.where(first, parts[s], turned[s + 1]) for s in (0, 2)], axis=1),
+        jnp.concatenate([jnp.where(first, turned[s], parts[s + 1]) for s in (0, 2)], axis=1),
+    ]
+    high, low = split(jnp.concatenate(field, axis=0))
+    return dot(high, hz[0]) + dot(high, hz[1]) + dot(low, hz[0])
+
+
+def store(done, last, last_factor, hz, o_hbm, line, sems):
+    ready = pl.ds(0, 15)
+    bulk = pltpu.make_async_copy(done.at[:, ready], o_hbm.at[:, ready], sems.at[0])
+    bulk.start()
+    res = z_line([last[s] for s in range(4)], hz)
+    for f in range(2):
+        line[f] = res[128 * f : 128 * (f + 1)] * last_factor[...]
+    tail = pltpu.make_async_copy(line, o_hbm.at[:, 15], sems.at[1])
+    tail.start()
+    bulk.wait()
+    tail.wait()
+
+
 def kernel(
-    x_hbm, sx_hbm, sy_hbm, sz_hbm, h_hbm, hz_hbm, out,
+    x_hbm, sx_hbm, sy_hbm, sz_hbm, h_hbm, hz_hbm, out, last, last_factor, hz_out,
     xin, h, hz, xo, zr, yr, yo, pr, fw, via, sx, sy, sz, sycol, factor,
-    in_sem, tab_sem, sym_sem, z_send, z_recv, xy_send, xy_recv, p_send, p_recv, f_send, f_recv, v_sem, near, far, row, column,
+    in_sem, tab_sem, sym_sem, sent, z_recv, xy_recv, p_recv, f_recv, v_recv, near, far, row, column,
 ):
     n = lax.axis_index("north")
     d = lax.axis_index("deep")
@@ -49,13 +78,16 @@
     qx, qy = q % SIDE, q // SIDE
     group = 16 // PIECES
 
-    def table_copy(rel):
-        side = jnp.where(rel == 1, 1 - half, half)
-        rows = pl.ds(pl.multiple_of(side * 256, 256), 256)
-        return pltpu.make_async_copy(h_hbm.at[:, rows], h.at[:, rows], tab_sem.at[rel])
-
-    hz_copy = pltpu.make_async_copy(hz_hbm, hz, tab_sem.at[2])
-    table_copy(1).start()
+    def table_rows(rel, first, count):
+        side = 1 - half if rel == 1 else half
+        return pl.ds(pl.multiple_of(side * 256 + first, 128), count)
+
+    def table_copy(k):
+        rows = table_rows(*((0, 0, 256), (1, 0, 128), (1, 128, 128))[k])
+        return pltpu.make_async_copy(h_hbm.at[:, rows], h.at[:, rows], tab_sem.at[k])
+
+    hz_copy = pltpu.make_async_copy(hz_hbm, hz, sym_sem)
+    table_copy(2).start()
 
     def in_copy(i, f):
         return pltpu.make_async_copy(x_hbm.at[f, pl.ds(2 * i, 2)], xin.at[pl.ds(2 * i, 2), f], in_sem.at[min(i, 1)])
@@ -63,9 +95,9 @@
     for f in range(2):
         in_copy(0, f).start()
     symbol_copies = [
-        pltpu.make_async_copy(sx_hbm, sx, sym_sem.at[0]),
-        pltpu.make_async_copy(sy_hbm, sy, sym_sem.at[1]),
-        pltpu.make_async_copy(sz_hbm, sz, sym_sem.at[2]),
+        pltpu.make_async_copy(sx_hbm, sx, sym_sem),
+        pltpu.make_async_copy(sy_hbm, sy, sym_sem),
+        pltpu.make_async_copy(sz_hbm, sz, sym_sem),
     ]
 
     def plane_chip(step):
@@ -102,54 +134,44 @@
         return pltpu.make_async_remote_copy(
             src_ref=xo.at[1, c, :, part],
             dst_ref=zr.at[c, :, part],
-            send_sem=z_send,
+            send_sem=sent,
             recv_sem=z_recv.at[c, i // group],
             device_id=across,
             device_id_type=MESH,
         )
 
 
-    def x_half(i, rel):
-        value = xin[pl.ds(2 * i, 2)].reshape(256, 512)
-        high, low = split(value)
-        side = jnp.where(rel == 1, 1 - half, half)
-        rows = pl.ds(pl.multiple_of(side * 256, 256), 256)
+    def x_rows(i, high, low, rel, first, count):
+        rows = table_rows(rel, first, count)
         a_high, a_low = h[0, rows, :], h[1, rows, :]
         res = dot(a_high, high, 1) + dot(a_low, high, 1) + dot(a_high, low, 1)
-        res = res.reshape(PLANE, 2, 8, 256)
-        for c in range(2):
+        for k in range(count // 128):
+            part = res[128 * k : 128 * (k + 1)].reshape(PLANE, 8, 256)
             for y in range(2):
-                xo[rel, c, :, 2 * i + y] = res[:, c, :, 128 * y : 128 * (y + 1)]
-
-    def x_pair(i):
+                xo[rel, first // 128 + k, :, 2 * i + y] = part[:, :, 128 * y : 128 * (y + 1)]
+
+    def x_halves(i, *parts):
         high, low = split(xin[pl.ds(2 * i, 2)].reshape(256, 512))
-        for rel in (1, 0):
-            side = jnp.where(rel == 1, 1 - half, half)
-            rows = pl.ds(pl.multiple_of(side * 256, 256), 256)
-            a_high, a_low = h[0, rows, :], h[1, rows, :]
-            res = dot(a_high, high, 1) + dot(a_low, high, 1) + dot(a_high, low, 1)
-            res = res.reshape(PLANE, 2, 8, 256)
-            for c in range(2):
-                for y in range(2):
-                    xo[rel, c, :, 2 * i + y] = res[:, c, :, 128 * y : 128 * (y + 1)]
+        for part in parts:
+            x_rows(i, high, low, *part)
 
     def x_step(i, carry):
-        x_pair(i)
+        x_halves(i, (1, 0, 256), (0, 0, 256))
         z_copy(0, 2 * i, 2).start()
         return carry
 
     first_copy = pltpu.make_async_remote_copy(
         src_ref=xo.at[1, 1, :, pl.ds(0, 2)],
         dst_ref=via,
-        send_sem=v_sem.at[0],
-        recv_sem=v_sem.at[1],
+        send_sem=sent,
+        recv_sem=v_recv,
         device_id=mate,
         device_id_type=MESH,
     )
     onward_copy = pltpu.make_async_remote_copy(
         src_ref=via,
         dst_ref=zr.at[1, :, pl.ds(0, 2)],
-        send_sem=z_send,
+        send_sem=sent,
         recv_sem=z_recv.at[1, 0],
         device_id=beyond,
         device_id_type=MESH,
@@ -157,15 +179,16 @@
     def in_wait(planes, k):
         pltpu.make_async_copy(xin.at[planes], xin.at[planes], in_sem.at[k]).wait()
 
-    table_copy(1).wait()
+    table_copy(2).wait()
     in_wait(pl.ds(0, 2), 0)
+    table_copy(1).start()
     table_copy(0).start()
     for i in range(1, 8):
         for f in range(2):
             in_copy(i, f).start()
     for copy in [hz_copy, *symbol_copies]:
         copy.start()
-    x_half(0, 1)
+    x_halves(0, (1, 128, 128))
     pl.semaphore_wait(barrier, contacts)
     first_copy.start()
     @pl.when(middle)
@@ -173,11 +196,13 @@
         tell(near, mate)
         tell(near, beyond)
 
-    table_copy(0).wait()
-    x_half(0, 0)
+    table_copy(1).wait()
+    x_halves(0, (1, 0, 128))
     pl.semaphore_wait(near, 1)
     z_copy(0, 0, 2).start()
     pl.when(middle)(lambda: tell(far, across))
+    table_copy(0).wait()
+    x_halves(0, (0, 0, 256))
     in_wait(pl.ds(2, 14), 1)
     lax.fori_loop(1, 4, x_step, 0)
     sweep(row, qx, 1)
@@ -197,7 +222,7 @@
             pltpu.make_async_remote_copy(
                 src_ref=xo.at[0, c, to],
                 dst_ref=yr.at[c, n],
-                send_sem=xy_send,
+                send_sem=sent,
                 recv_sem=xy_recv.at[c],
                 device_id=(half * PLANE + to, d),
                 device_id_type=MESH,
@@ -216,7 +241,7 @@
                 pltpu.make_async_remote_copy(
                     src_ref=zr.at[c, to, part],
                     dst_ref=yr.at[c, from_across, part],
-                    send_sem=xy_send,
+                    send_sem=sent,
                     recv_sem=xy_recv.at[c],
                     device_id=(half * PLANE + to, d),
                     device_id_type=MESH,
@@ -234,7 +259,7 @@
         return pltpu.make_async_remote_copy(
             src_ref=ref.at[part],
             dst_ref=pr.at[c, source, part],
-            send_sem=p_send,
+            send_sem=sent,
             recv_sem=p_recv.at[c * 4 + j // LINES[c]],
             device_id=(n, to),
             device_id_type=MESH,
@@ -245,22 +270,30 @@
         return pltpu.make_async_remote_copy(
             src_ref=yo.at[c, d ^ 3, part],
             dst_ref=fw.at[c, part],
-            send_sem=f_send,
-            recv_sem=f_recv.at[c * 4 + i],
+            send_sem=sent,
+            recv_sem=f_recv.at[c],
             device_id=(n, d ^ 1),
             device_id_type=MESH,
         )
 
-    def onward(c, i):
-        to_twin(c, i).wait_recv()
-        for j in firsts(c):
-            p_copy(fw.at[c], d ^ 1, c, 2 * i + j, d ^ 2).start()
+    def onward(c):
+        whole = fw.at[c]
+        pltpu.make_async_remote_copy(
+            src_ref=whole, dst_ref=whole, send_sem=sent, recv_sem=f_recv.at[c], device_id=twin, device_id_type=MESH
+        ).wait_recv()
+
+        def pair(i, carry):
+            for j in firsts(c):
+                p_copy(fw.at[c], d ^ 1, c, 2 * i + j, d ^ 2).start()
+            return carry
+
+        lax.fori_loop(0, 4, pair, 0)
 
     def along_y(c):
         pltpu.make_async_remote_copy(
             src_ref=yr.at[c, pl.ds(0, 30)],
             dst_ref=yr.at[c, pl.ds(0, 30)],
-            send_sem=xy_send,
+            send_sem=sent,
             recv_sem=xy_recv.at[c],
             device_id=across,
             device_id_type=MESH,
@@ -274,6 +307,7 @@
                 rows = pl.ds(part * 256, 256)
                 a_high, a_low = h[0, rows, :], h[1, rows, :]
                 res = dot(a_high, high) + dot(a_low, high) + dot(a_high, low)
+                res = jnp.swapaxes(res.reshape(2, PLANE, 8, 256), 0, 1).reshape(256, 256)
                 for k in range(2):
                     for s in range(2):
                         yo[c, 2 * part + s, 2 * i + k] = res[128 * s : 128 * (s + 1), 128 * k : 128 * (k + 1)]
@@ -283,47 +317,36 @@
                 p_copy(yo.at[c, d ^ 1], d, c, 2 * i + j, d ^ 1).start()
                 p_copy(yo.at[c, d ^ 2], d, c, 2 * i + j, d ^ 2).start()
 
-            @pl.when(i > 0)
-            def _():
-                onward(c, i - 1)
-
             return carry
 
         lax.fori_loop(0, 4, pair, 0)
-        onward(c, 3)
+        onward(c)
+
+    def line_factor(c, j):
+        symbol = (sx[n * 16 + c * 8 + j] + sycol[...]) + sz[...]
+        return (1.0 - 0.2 * symbol) / (1.0 + 0.2 * symbol)
+
+    def line_wait(c, j):
+        whole = pr.at[c, pl.ds(0, 3), pl.ds(0, LINES[c])]
+        pltpu.make_async_remote_copy(
+            src_ref=whole,
+            dst_ref=whole,
+            send_sem=sent,
+            recv_sem=p_recv.at[c * 4 + j // LINES[c]],
+            device_id=across,
+            device_id_type=MESH,
+        ).wait_recv()
 
     def along_z(c):
-        first = lax.broadcasted_iota(jnp.int32, (128, 128), 1) < 64
-
         def line(j, carry):
-            symbol = (sx[n * 16 + c * 8 + j] + sycol[...]) + sz[...]
-            factor[...] = (1.0 - 0.2 * symbol) / (1.0 + 0.2 * symbol)
-
-            @pl.when(j % LINES[c] == 0)
-            def _():
-                whole = pr.at[c, pl.ds(0, 3), pl.ds(0, LINES[c])]
-                pltpu.make_async_remote_copy(
-                    src_ref=whole,
-                    dst_ref=whole,
-                    send_sem=p_send,
-                    recv_sem=p_recv.at[c * 4 + j // LINES[c]],
-                    device_id=across,
-                    device_id_type=MESH,
-                ).wait_recv()
-
-            parts = [pr[c, s, j] for s in range(4)]
-            turned = [pltpu.roll(p, 64, 1) for p in parts]
-            field = [
-                jnp.concatenate([jnp.where(first, parts[s], turned[s + 1]) for s in (0, 2)], axis=1),
-                jnp.concatenate([jnp.where(first, turned[s], parts[s + 1]) for s in (0, 2)], axis=1),
-            ]
-            high, low = split(jnp.concatenate(field, axis=0))
-            res = dot(high, hz[0]) + dot(high, hz[1]) + dot(low, hz[0])
+            factor[...] = line_factor(c, j)
+            pl.when(j % LINES[c] == 0)(lambda: line_wait(c, j))
+            res = z_line([pr[c, s, j] for s in range(4)], hz)
             for f in range(2):
                 out[f, c * 8 + j] = res[128 * f : 128 * (f + 1)] * factor[...]
             return carry
 
-        lax.fori_loop(0, 8, line, 0)
+        lax.fori_loop(0, 8 - c, line, 0)
 
     xy_own(0)
     xy_relay(0)
@@ -331,6 +354,7 @@
     for copy in symbol_copies:
         copy.wait()
     hz_copy.wait()
+    hz_out[...] = hz[...]
     along = sy[pl.ds(d, 1), :]
     sycol[...] = jnp.concatenate([jnp.transpose(jnp.broadcast_to(along, (128, 128)))] * 2, axis=1)
     along_y(0)
@@ -338,27 +362,36 @@
     along_y(1)
     along_z(0)
     along_z(1)
+    last_factor[...] = line_factor(1, 7)
+    line_wait(1, 7)
+    for s in range(4):
+        last[s] = pr[1, s, 7]
 
     def drain(ref, sem):
         pltpu.make_async_remote_copy(
             src_ref=ref, dst_ref=ref, send_sem=sem, recv_sem=p_recv.at[0], device_id=across, device_id_type=MESH
         ).wait_send()
 
-    first_copy.wait_send()
-    drain(zr, z_send)
+    drain(via, sent)
+    drain(zr, sent)
     for c in range(2):
-        drain(yr.at[c, pl.ds(0, 30)], xy_send)
-        drain(pr.at[c, pl.ds(0, 3)], p_send)
-        drain(fw.at[c], f_send)
+        drain(yr.at[c, pl.ds(0, 30)], sent)
+        drain(pr.at[c, pl.ds(0, 3)], sent)
+        drain(fw.at[c], sent)
 
 
 def local(forcing, symbol_x, symbol_y, symbol_z):
     lines = jnp.transpose(forcing, (0, 2, 3, 1))
-    return pl.pallas_call(
+    parts = pl.pallas_call(
         kernel,
-        out_shape=jax.ShapeDtypeStruct((2, 16, 128, 256), F32),
+        out_shape=[
+            jax.ShapeDtypeStruct((2, 16, 128, 256), F32),
+            jax.ShapeDtypeStruct((4, 128, 128), F32),
+            jax.ShapeDtypeStruct((128, 256), F32),
+            jax.ShapeDtypeStruct((2, 256, 256), BF16),
+        ],
         in_specs=[pl.BlockSpec(memory_space=pltpu.HBM)] * 6,
-        out_specs=pl.BlockSpec(memory_space=pltpu.VMEM),
+        out_specs=[pl.BlockSpec(memory_space=pltpu.VMEM)] * 4,
         scratch_shapes=[
             pltpu.VMEM((16, 2, 64, 512), F32),
             pltpu.VMEM((2, 512, 512), BF16),
@@ -377,16 +410,13 @@
             pltpu.VMEM((128, 256), F32),
             pltpu.SemaphoreType.DMA((2,)),
             pltpu.SemaphoreType.DMA((3,)),
-            pltpu.SemaphoreType.DMA((3,)),
+            pltpu.SemaphoreType.DMA,
             pltpu.SemaphoreType.DMA,
             pltpu.SemaphoreType.DMA((2, PIECES)),
-            pltpu.SemaphoreType.DMA,
+            pltpu.SemaphoreType.DMA((2,)),
+            pltpu.SemaphoreType.DMA((12,)),
             pltpu.SemaphoreType.DMA((2,)),
             pltpu.SemaphoreType.DMA,
-            pltpu.SemaphoreType.DMA((12,)),
-            pltpu.SemaphoreType.DMA,
-            pltpu.SemaphoreType.DMA((8,)),
-            pltpu.SemaphoreType.DMA((2,)),
             pltpu.SemaphoreType.REGULAR,
             pltpu.SemaphoreType.REGULAR,
             pltpu.SemaphoreType.REGULAR((2,)),
@@ -404,11 +434,21 @@
                 symbol_x,
                 symbol_y.reshape(4, 128),
                 symbol_z.reshape(1, 256),
-                jnp.asarray(table(512)),
+                jnp.asarray(by_chunk(table(512))),
                 jnp.asarray(table(256)),
             )
         )
     )
+
+    return pl.pallas_call(
+        store,
+        out_shape=jax.ShapeDtypeStruct((2, 16, 128, 256), F32),
+        in_specs=[pl.BlockSpec(memory_space=pl.ANY)] + [pl.BlockSpec(memory_space=pltpu.VMEM)] * 3,
+        out_specs=pl.BlockSpec(memory_space=pltpu.HBM),
+        scratch_shapes=[pltpu.VMEM((2, 128, 256), F32), pltpu.SemaphoreType.DMA((2,))],
+        compiler_params=pltpu.CompilerParams(vmem_limit_bytes=8 * 2**20),
+        name="store",
+    )(*parts)
 
 
 def solution(mesh):

time: 97.7 us -> 97.1 us (level)
  local copies, waits for them, and re-layouts: 2.02 us -> 0 us
  Pallas kernels: 95.5 us -> 96.9 us
    unnamed x1 -> x0, local copies, waits for them, and re-layouts: 2.02 us -> none
    pallas_call x1 -> x2, Pallas kernels: 95.5 us -> 96.9 us  [the longest x1 94.9 us: local(): pl.pallas_call(kernel, out_shape=[jax.ShapeDtypeStruct((2, 16, 128, 256),...]
where the time goes in v3:
time: 97.1 us; the launch traced here: 97 us
  Pallas kernels  96.9 us (100%)
    pallas_call x1, Pallas kernels, local(): pl.pallas_call(kernel, out_shape=[jax.ShapeDtypeStruct((2, 16, 128, 256),...  94.9 us
    pallas_call x1, Pallas kernels, local(): pl.pallas_call(store, out_shape=jax.ShapeDtypeStruct((2, 16, 128, 256), F...  2.05 us

profile of v3, /device:TPU:1, one launch (start us, length us, event | category | flops | bytes accessed | tf_op | source)
XLA Modules:
  0.0 97.0 jit_solution(14320826378013845733)
XLA Ops:
  0.0 94.9 %transform.1 = (f32[2,16,128,256]{3,2,1,0:T(8,128)S(1)}, f32[4,128,128]{2,1,0:T(8,128)S(1)}, f32[128,256]{1,0:T(8,128)S(1)}, bf16[2,256,256]{2,1,0:T(8,128)(2,1)S(1)}) custom-call(f32[2,16,64,512]{3,2,1,0:T(8,128)} %bitcast.3, f32[512]{0:T(512)} %sx_hbm.1, f32[4,128]{1,0:T(4,128)} %bitcast.4, f32[1,256]{1,0:T(1,128)} %bitcast.5, ...), custom_call_target="tpu_custom_call" | custom-call | tf_op jit(solution)/shard_map/transform/pallas_call | solution.py:385
  94.9 2.1 %store.1 = f32[2,16,128,256]{3,2,1,0:T(8,128)} custom-call(f32[2,16,128,256]{3,2,1,0:T(8,128)S(1)} %get-tuple-element.9.done, f32[4,128,128]{2,1,0:T(8,128)S(1)} %get-tuple-element.10.last, f32[128,256]{1,0:T(8,128)S(1)} %get-tuple-element.11.last_factor, bf16[2,256,256]{2,1,0:T(8,128)(2,1)S(1)} %get-tuple-element.12.hz), custom_call_target="tpu_custom_call" | custom-call | tf_op jit(solution)/shard_map/store/pallas_call | solution.py:443

commit v4 on v3

--- a/solution.py
+++ b/solution.py
@@ -15,7 +15,7 @@
 PLANE = SIDE * SIDE
 STEPS = ((1, 0), (0, 1), (3, 0), (0, 3), (1, 1), (3, 3), (1, 3), (3, 1), (2, 0), (0, 2), (2, 1), (1, 2), (2, 3), (3, 2), (2, 2))
 LINE = tuple(step for step in STEPS if 0 in step)
-PIECES = 4
+PIECES = 2
 
 LINES = (2, 1)
 
@@ -212,7 +212,7 @@
     first_copy.wait_recv()
     pl.when(outer)(lambda: pl.semaphore_wait(far, 1))
     onward_copy.start()
-    z_copy(1, 2, 2).start()
+    z_copy(1, 2, group - 2).start()
     for g in range(1, PIECES):
         z_copy(1, g * group, group).start()
 

time: 97.1 us -> 97.1 us (level)
  no operation moved by 1% of the time
where the time goes in v4:
time: 97.1 us; the launch traced here: 96.9 us
  Pallas kernels  96.9 us (100%)
    pallas_call x1, Pallas kernels, local(): pl.pallas_call(kernel, out_shape=[jax.ShapeDtypeStruct((2, 16, 128, 256),...  94.9 us
    pallas_call x1, Pallas kernels, local(): pl.pallas_call(store, out_shape=jax.ShapeDtypeStruct((2, 16, 128, 256), F...  2.05 us

profile of v4, /device:TPU:1, one launch (start us, length us, event | category | flops | bytes accessed | tf_op | source)
XLA Modules:
  0.0 96.9 jit_solution(17678235782350887640)
XLA Ops:
  0.0 94.9 %transform.1 = (f32[2,16,128,256]{3,2,1,0:T(8,128)S(1)}, f32[4,128,128]{2,1,0:T(8,128)S(1)}, f32[128,256]{1,0:T(8,128)S(1)}, bf16[2,256,256]{2,1,0:T(8,128)(2,1)S(1)}) custom-call(f32[2,16,64,512]{3,2,1,0:T(8,128)} %bitcast.3, f32[512]{0:T(512)} %sx_hbm.1, f32[4,128]{1,0:T(4,128)} %bitcast.4, f32[1,256]{1,0:T(1,128)} %bitcast.5, ...), custom_call_target="tpu_custom_call" | custom-call | tf_op jit(solution)/shard_map/transform/pallas_call | solution.py:385
  94.9 2.1 %store.1 = f32[2,16,128,256]{3,2,1,0:T(8,128)} custom-call(f32[2,16,128,256]{3,2,1,0:T(8,128)S(1)} %get-tuple-element.9.done, f32[4,128,128]{2,1,0:T(8,128)S(1)} %get-tuple-element.10.last, f32[128,256]{1,0:T(8,128)S(1)} %get-tuple-element.11.last_factor, bf16[2,256,256]{2,1,0:T(8,128)(2,1)S(1)} %get-tuple-element.12.hz), custom_call_target="tpu_custom_call" | custom-call | tf_op jit(solution)/shard_map/store/pallas_call | solution.py:443
